TPU v7x, 256 devices: a whole 4x4x8 slice. The times are simulated.
256 devices in a mesh: unit: 4 (over x), replica: 16 (over z, core), model: 4 (over y).
Axes of the slice: x: 4, y: 4, z: 8, core: 2. Of those that a mesh axis runs over, the one named last changes fastest.
Arguments:
- slope_up: float32 [64, 768, 3072], P(('unit', 'replica'), None, 'model'), parts along dimension 0, may hold values from -0.875 to 0.875
- slope_down: float32 [64, 3072, 768], P(('unit', 'replica'), 'model'), parts along dimension 0, may hold values from -0.875 to 0.875
- slope_query: float32 [64, 768, 768], P(('unit', 'replica'), None, 'model'), parts along dimension 0, may hold values from -0.875 to 0.875
- slope_key: float32 [64, 768, 768], P(('unit', 'replica'), None, 'model'), parts along dimension 0, may hold values from -0.875 to 0.875
- slope_value: float32 [64, 768, 768], P(('unit', 'replica'), None, 'model'), parts along dimension 0, may hold values from -0.875 to 0.875
- slope_mixed: float32 [64, 768, 768], P(('unit', 'replica'), 'model'), parts along dimension 0, may hold values from -0.875 to 0.875
- slope_norm: float32 [64, 768], P(('unit', 'replica')), parts along dimension 0, may hold values from -8 to 8
- param_up: float32 [3072, 3072], P(('unit', 'replica'), 'model'), parts along dimension 0, may hold values from -0.21875 to 0.21875
- param_down: float32 [12288, 768], P(('unit', 'model'), 'replica'), parts along dimension 0, may hold values from -0.109375 to 0.109375
- param_query: float32 [3072, 768], P(('unit', 'replica'), 'model'), parts along dimension 0, may hold values from -0.21875 to 0.21875
- param_key: float32 [3072, 768], P(('unit', 'replica'), 'model'), parts along dimension 0, may hold values from -0.21875 to 0.21875
- param_value: float32 [3072, 768], P(('unit', 'replica'), 'model'), parts along dimension 0, may hold values from -0.21875 to 0.21875
- param_mixed: float32 [3072, 768], P(('unit', 'model'), 'replica'), parts along dimension 0, may hold values from -0.21875 to 0.21875
- param_norm: float32 [3072], P(('unit', 'replica')), parts along dimension 0, may hold values from 0.25 to 1.75
Outputs:
- half_up: bfloat16 [3072, 3072], P('unit', 'model'), parts along dimension 0
- half_down: bfloat16 [12288, 768], P(('unit', 'model')), parts along dimension 0
- half_query: bfloat16 [3072, 768], P('unit', 'model'), parts along dimension 0
- half_key: bfloat16 [3072, 768], P('unit', 'model'), parts along dimension 0
- half_value: bfloat16 [3072, 768], P('unit', 'model'), parts along dimension 0
- half_mixed: bfloat16 [3072, 768], P(('unit', 'model')), parts along dimension 0
- half_norm: bfloat16 [3072], P('unit'), parts along dimension 0
- next_up: float32 [3072, 3072], P(('unit', 'replica'), 'model'), parts along dimension 0
- next_down: float32 [12288, 768], P(('unit', 'model'), 'replica'), parts along dimension 0
- next_query: float32 [3072, 768], P(('unit', 'replica'), 'model'), parts along dimension 0
- next_key: float32 [3072, 768], P(('unit', 'replica'), 'model'), parts along dimension 0
- next_value: float32 [3072, 768], P(('unit', 'replica'), 'model'), parts along dimension 0
- next_mixed: float32 [3072, 768], P(('unit', 'model'), 'replica'), parts along dimension 0
- next_norm: float32 [3072], P(('unit', 'replica')), parts along dimension 0
There are 4 independent parts, one for each index of `unit`. A program takes and returns all parts, laid end to end along the dimension named above; each array names one. Nothing has to cross between parts.
All inputs are finite; a program needn't handle non-finite values.
Results may differ from a plain program's by a relative error of at most 0.001.
Values may be sent and summed in bfloat16 or wider, within the bound.
No kernel may reach another device: no remote copies, remote signals or barrier semaphores. Data moves between devices by JAX's collectives and lax.ppermute only.
A program may use at most 64 MiB of HBM per device.

v0:
```python
import jax
import jax.numpy as jnp
from jax import lax
from jax.sharding import PartitionSpec as P

learn_rate = 0.3


def split_up(array, dim, size):
    lengths = array.shape
    parts = array.reshape(*lengths[:dim], size, lengths[dim] // size, *lengths[dim + 1 :])
    return jnp.moveaxis(parts, dim, 0)


def sum_together(arrays, axis, dims):
    size = lax.axis_size(axis)
    parts = [split_up(a, dim, size) for a, dim in zip(arrays, dims)]
    lines = jnp.concatenate([b.reshape(size, -1) for b in parts], axis=1)
    width = max(16, -(-lines.shape[1] // 1024) * 8)
    lines = jnp.pad(lines, ((0, 0), (0, width * 128 - lines.shape[1]))).reshape(-1, 128)
    vector, at, finished = (lax.psum_scatter(lines, axis, tiled=True).reshape(-1), 0, [])
    for b in parts:
        part = b[0]
        finished.append(vector[at : at + part.size].reshape(part.shape))
        at += part.size
    return tuple(finished)


def rows_first(arrays, axis, dims):
    turned = [jnp.moveaxis(a, dim, 0) for a, dim in zip(arrays, dims)]
    both = jnp.concatenate([t.reshape(len(t), -1) for t in turned], axis=1)
    out, at, finished = (lax.all_gather(both, axis, axis=0, tiled=True), 0, [])
    for t, dim in zip(turned, dims):
        slab = out[:, at : at + t[0].size].reshape(-1, *t.shape[1:])
        finished.append(jnp.moveaxis(slab, 0, dim))
        at += t[0].size
    return tuple(finished)


def shards(
    slope_up,
    slope_down,
    slope_query,
    slope_key,
    slope_value,
    slope_mixed,
    slope_norm,
    param_up,
    param_down,
    param_query,
    param_key,
    param_value,
    param_mixed,
    param_norm,
):
    mean_up, mean_down, mean_query, mean_key, mean_value, mean_mixed, mean_norm = sum_together(
        (
            slope_up[0],
            slope_down[0],
            slope_query[0],
            slope_key[0],
            slope_value[0],
            slope_mixed[0],
            slope_norm[0],
        ),
        "replica",
        (0, 1, 0, 0, 0, 1, 0),
    )
    mean_rate = lax.axis_size("replica") ** (-0.5)
    mean_up = mean_up * mean_rate
    mean_down = mean_down * mean_rate
    mean_query = mean_query * mean_rate
    mean_key = mean_key * mean_rate
    mean_value = mean_value * mean_rate
    mean_mixed = mean_mixed * mean_rate
    mean_norm = mean_norm * mean_rate
    next_up = param_up - learn_rate * mean_up
    next_down = param_down - learn_rate * mean_down
    next_query = param_query - learn_rate * mean_query
    next_key = param_key - learn_rate * mean_key
    next_value = param_value - learn_rate * mean_value
    next_mixed = param_mixed - learn_rate * mean_mixed
    next_norm = param_norm - learn_rate * mean_norm
    half_up, half_down, half_query, half_key, half_value, half_mixed, half_norm = rows_first(
        (
            next_up.astype(jnp.bfloat16),
            next_down.astype(jnp.bfloat16),
            next_query.astype(jnp.bfloat16),
            next_key.astype(jnp.bfloat16),
            next_value.astype(jnp.bfloat16),
            next_mixed.astype(jnp.bfloat16),
            next_norm.astype(jnp.bfloat16),
        ),
        "replica",
        (0, 1, 0, 0, 0, 1, 0),
    )
    return (
        half_up,
        half_down,
        half_query,
        half_key,
        half_value,
        half_mixed,
        half_norm,
        next_up,
        next_down,
        next_query,
        next_key,
        next_value,
        next_mixed,
        next_norm,
    )


def solution(mesh):
    placed = (
        P(("unit", "replica"), None, "model"),
        P(("unit", "replica"), "model", None),
        P(("unit", "replica"), None, "model"),
        P(("unit", "replica"), None, "model"),
        P(("unit", "replica"), None, "model"),
        P(("unit", "replica"), "model", None),
        P(("unit", "replica"), None),
        P(("unit", "replica"), "model"),
        P(("unit", "model"), "replica"),
        P(("unit", "replica"), "model"),
        P(("unit", "replica"), "model"),
        P(("unit", "replica"), "model"),
        P(("unit", "model"), "replica"),
        P(("unit", "replica")),
    )
    return jax.shard_map(
        shards,
        mesh=mesh,
        in_specs=placed,
        out_specs=(
            P("unit", "model"),
            P(("unit", "model"), None),
            P("unit", "model"),
            P("unit", "model"),
            P("unit", "model"),
            P(("unit", "model"), None),
            P("unit"),
            P(("unit", "replica"), "model"),
            P(("unit", "model"), "replica"),
            P(("unit", "replica"), "model"),
            P(("unit", "replica"), "model"),
            P(("unit", "replica"), "model"),
            P(("unit", "model"), "replica"),
            P(("unit", "replica")),
        ),
        check_vma=False,
    )
```

profile of v0, /device:TPU:1, one launch (start us, length us, event | category | flops | bytes accessed | tf_op | source)
XLA Modules:
  0.0 258.9 jit_solution(8501076146839965189)
XLA Ops:
  7.2 1.9 reshape_reshape_squeeze.12
  9.1 1.6 constant_dynamic-update-slice_fusion.6
  10.7 2.0 copy.69
  12.7 4.1 %copy.70 = f32[16,768,48]{2,1,0:T(8,128)} copy(f32[16,768,48]{1,2,0:T(8,128)S(1)} %bitcast.19) | data formatting | bytes 4718592 | tf_op jit(solution)/shard_map/transpose | solution.py:12
  16.8 7.3 %reshape.76 = f32[16,36864]{1,0:T(8,128)S(1)} reshape(f32[16,768,48]{2,1,0:T(8,128)} %copy.70) | data formatting | bytes 4718592 | tf_op jit(solution)/shard_map/reshape | solution.py:18
  24.1 1.3 copy.71
  25.5 1.1 reshape_reshape_squeeze.13
  26.6 1.3 copy.72
  27.9 1.1 reshape_reshape_squeeze.14
  29.0 1.3 copy.73
  30.4 1.1 reshape_reshape_squeeze.15
  31.5 1.3 copy.74
  32.8 1.7 copy.75
  34.5 3.5 %reshape.77 = f32[16,9216]{1,0:T(8,128)} reshape(f32[16,192,48]{2,1,0:T(8,128)} %copy.75) | data formatting | bytes 1179648 | tf_op jit(solution)/shard_map/reshape | solution.py:18
  38.1 1.6 constant_dynamic-update-slice_fusion.5
  39.7 0.9 constant_dynamic-update-slice_fusion.4
  40.6 0.9 constant_dynamic-update-slice_fusion.3
  41.4 0.9 constant_dynamic-update-slice_fusion.2
  42.3 0.9 constant_dynamic-update-slice_fusion.1
  43.2 0.6 constant_dynamic-update-slice_fusion
  43.8 6.4 %pad.4 = f32[16,111616]{1,0:T(8,128)} pad(f32[16,110640]{1,0:T(8,128)} %constant_dynamic-update-slice_fusion, f32[]{:T(128)} %constant.8.clone.1), padding=0_0x0_976 | pad | bytes 14224388 | tf_op jit(solution)/shard_map/jit(_pad)/pad | solution.py:20
  50.1 5.5 %reshape.78 = f32[13952,128]{1,0:T(8,128)} reshape(f32[16,111616]{1,0:T(8,128)} %pad.4) | data formatting | bytes 14286848 | tf_op jit(solution)/shard_map/reshape | solution.py:20
  55.8 0.5 copy-done.12
  56.3 0.6 dynamic-slice
  57.5 132.0 %all-reduce.4.cloned.1.call-done = f32[13952,128]{1,0:T(8,128)} async-done(((f32[13952,128]{1,0:T(8,128)}), f32[13952,128]{1,0:T(8,128)}) %all-reduce.4.cloned.1.call-update) | async-done | bytes 7143440
  189.5 1.0 dynamic-slice_multiply_fusion
  190.6 0.2 mul.64
  190.7 0.1 copy.76
  190.9 0.9 dynamic-slice_multiply_fusion.2
  192.0 0.1 mul.73
  192.2 1.1 dynamic-slice_bitcast_fusion
  193.3 0.5 convert_bitcast_fusion.2
  193.8 0.1 copy.78
  193.9 0.7 fusion.5
  194.6 0.7 convert_bitcast_fusion
  195.2 0.6 fusion.4
  195.9 0.6 convert_bitcast_fusion.1
  196.5 0.6 fusion.2
  197.2 0.8 concatenate.7
  198.0 42.8 %all-gather.2.cloned.1.call-done = bf16[768,2305]{1,0:T(8,128)(2,1)} async-done(((bf16[48,2305]{1,0:T(8,128)(2,1)}), bf16[768,2305]{1,0:T(8,128)(2,1)}) %all-gather.2.cloned.1.call-update) | async-done | bytes 3540496 | tf_op jit(solution)/shard_map/all_gather | solution.py:32
  240.8 2.8 %slice_bitcast_fusion = (bf16[768,768]{0,1:T(8,128)(2,1)S(1)}, bf16[768,768]{1,0:T(8,128)(2,1)}) fusion(bf16[768,2305]{1,0:T(8,128)(2,1)} %all-gather.2.cloned.1.call-done), kind=kLoop, calls=%fused_computation | loop fusion | bytes 4718592 | tf_op jit(solution)/shard_map/transpose | solution.py:35
  243.6 1.4 copy.79
  245.0 1.9 slice_bitcast_fusion.1
  246.9 0.9 copy.80
  247.8 0.9 copy.81
  248.7 0.9 copy.82
  249.5 0.9 copy.83
  250.4 1.7 slice_reduce_fusion
  (36 shorter events, 0.6 us)
Async XLA Ops:
  7.2 182.3 %all-reduce.4.cloned.1.call-start = ((), (), s32[]{:S(2)}) async-start(), calls=%async_computation.1 | async-start | bytes 14286848
  24.1 13.9 %copy-start.10 = (f32[1,768]{1,0:T(1,128)S(1)}, f32[1,768]{1,0:T(1,128)}, u32[]{:S(2)}) copy-start(f32[1,768]{1,0:T(1,128)} %param.20) | copy-start | bytes 9220
  34.5 5.1 %copy-start = (f32[16,9216]{1,0:T(8,128)S(1)}, f32[16,9216]{1,0:T(8,128)}, u32[]{:S(2)}) copy-start(f32[16,9216]{1,0:T(8,128)} %reshape_reshape_squeeze.13) | copy-start | bytes 1769476
  34.5 6.0 %copy-start.1 = (f32[16,9216]{1,0:T(8,128)S(1)}, f32[16,9216]{1,0:T(8,128)}, u32[]{:S(2)}) copy-start(f32[16,9216]{1,0:T(8,128)} %reshape_reshape_squeeze.14) | copy-start | bytes 1769476
  38.1 3.3 %copy-start.2 = (f32[16,9216]{1,0:T(8,128)S(1)}, f32[16,9216]{1,0:T(8,128)}, u32[]{:S(2)}) copy-start(f32[16,9216]{1,0:T(8,128)} %reshape_reshape_squeeze.15) | copy-start | bytes 1769476
  38.1 4.2 %copy-start.3 = (f32[16,9216]{1,0:T(8,128)S(1)}, f32[16,9216]{1,0:T(8,128)}, u32[]{:S(2)}) copy-start(f32[16,9216]{1,0:T(8,128)} %reshape.77) | copy-start | bytes 1769476
  55.6 0.7 copy-start.12
  55.6 137.6 %copy-start.11 = (f32[48]{0:T(128)S(1)}, f32[48]{0:T(128)}, u32[]{:S(2)}) copy-start(f32[48]{0:T(128)} %param.27) | copy-start | bytes 580
  55.6 138.3 %copy-start.4 = (f32[48,768]{1,0:T(8,128)S(1)}, f32[48,768]{1,0:T(8,128)}, u32[]{:S(2)}) copy-start(f32[48,768]{1,0:T(8,128)} %param.21) | copy-start | bytes 442372
  55.6 138.9 %copy-start.5 = (f32[768,48]{0,1:T(8,128)S(1)}, f32[768,48]{0,1:T(8,128)}, u32[]{:S(2)}) copy-start(f32[768,48]{0,1:T(8,128)} %param.22) | copy-start | bytes 442372
  55.6 139.6 %copy-start.6 = (f32[48,192]{1,0:T(8,128)S(1)}, f32[48,192]{1,0:T(8,128)}, u32[]{:S(2)}) copy-start(f32[48,192]{1,0:T(8,128)} %param.23) | copy-start | bytes 110596
  55.6 140.2 %copy-start.7 = (f32[192,48]{0,1:T(8,128)S(1)}, f32[192,48]{0,1:T(8,128)}, u32[]{:S(2)}) copy-start(f32[192,48]{0,1:T(8,128)} %param.26) | copy-start | bytes 110596
  55.7 140.8 %copy-start.8 = (f32[48,192]{1,0:T(8,128)S(1)}, f32[48,192]{1,0:T(8,128)}, u32[]{:S(2)}) copy-start(f32[48,192]{1,0:T(8,128)} %param.25) | copy-start | bytes 110596
  55.7 140.8 %copy-start.9 = (f32[48,192]{1,0:T(8,128)S(1)}, f32[48,192]{1,0:T(8,128)}, u32[]{:S(2)}) copy-start(f32[48,192]{1,0:T(8,128)} %param.24) | copy-start | bytes 110596
  55.7 185.1 %all-gather.2.cloned.1.call-start = ((), (), s32[]{:S(2)}) async-start(), calls=%async_computation | async-start | bytes 3969024 | tf_op jit(solution)/shard_map/all_gather | solution.py:32
Sparse Core Ops, SparseCore 0:
  55.8 133.6 all-reduce.3
  198.1 42.6 all-gather.1
where the time goes:
time: 259 us
  waiting for transfers between devices  175 us (68%)
  local copies, waits for them, and re-layouts  63.4 us (24%)
  between operations  14.9 us (6%)
  other arithmetic  5.71 us (2%)
    unnamed x3, waiting for transfers between devices  132 us
    all_gather x1, waiting for transfers between devices, rows_first(): out, at, finished = (lax.all_gather(both, axis, axis=0, tiled=True), 0, [])  42.8 us
    unnamed x43, local copies, waits for them, and re-layouts  20.1 us
    reshape x2, local copies, waits for them, and re-layouts, sum_together(): lines = jnp.concatenate([b.reshape(size, -1) for b in parts], axis=1)  10.8 us
    pad x1, local copies, waits for them, and re-layouts, sum_together(): jnp.pad(lines, ((0, 0), (0, width * 128 - lines.shape[1]))).reshape(-1, 128)  6.35 us
    transpose x2, local copies, waits for them, and re-layouts, split_up(): return jnp.moveaxis(parts, dim, 0)  5.77 us
    reshape x1, local copies, waits for them, and re-layouts, sum_together(): jnp.pad(lines, ((0, 0), (0, width * 128 - lines.shape[1]))).reshape(-1, 128)  5.49 us
    another operation x4, local copies, waits for them, and re-layouts, sum_together(): lines = jnp.concatenate([b.reshape(size, -1) for b in parts], axis=1)  5.22 us
  transfers between devices with their start and end apart: 2, of which 2 were waited for; matrix products, arithmetic and copies ran while one was open for 0% of the time, Pallas kernels for 0%

commit v1 on v0

--- a/solution.py
+++ b/solution.py
@@ -4,6 +4,13 @@
 from jax.sharding import PartitionSpec as P
 
 learn_rate = 0.3
+
+
+def swapped_in(block, name, dim):
+    devices = lax.axis_size(name)
+    blocks = jnp.stack([block for _ in range(devices)])
+    blocks = lax.all_to_all(blocks, name, split_axis=0, concat_axis=0)
+    return jnp.concatenate(blocks, axis=dim)
 
 
 def split_up(array, dim, size):
@@ -29,7 +36,7 @@
 def rows_first(arrays, axis, dims):
     turned = [jnp.moveaxis(a, dim, 0) for a, dim in zip(arrays, dims)]
     both = jnp.concatenate([t.reshape(len(t), -1) for t in turned], axis=1)
-    out, at, finished = (lax.all_gather(both, axis, axis=0, tiled=True), 0, [])
+    out, at, finished = (swapped_in(both, axis, 0), 0, [])
     for t, dim in zip(turned, dims):
         slab = out[:, at : at + t[0].size].reshape(-1, *t.shape[1:])
         finished.append(jnp.moveaxis(slab, 0, dim))

time: 259 us -> 305 us (1.18)
  blocking collectives: 0 us -> 93.4 us
  waiting for transfers between devices: 175 us -> 132 us
  local copies, waits for them, and re-layouts: 63.4 us -> 58.9 us
    all_to_all x0 -> x1, blocking collectives: none -> 93.4 us  [swapped_in(): blocks = lax.all_to_all(blocks, name, split_axis=0, concat_axis=0)]
    all_gather x1 -> x0, waiting for transfers between devices: 42.8 us -> none  [rows_first(): out, at, finished = (lax.all_gather(both, axis, axis=0, tiled=True), 0, [])]
    transpose x2, local copies, waits for them, and re-layouts: 4.68 us -> 1.55 us  [rows_first(): finished.append(jnp.moveaxis(slab, 0, dim))]
    unnamed x3 -> x2, waiting for transfers between devices: 132 us -> 132 us
  transfers between devices with their start and end apart: 2 -> 1, of which waited for: 2 -> 1; matrix products, arithmetic and copies ran while one was open for 0% -> 0% of each run, Pallas kernels for 0% -> 0%
where the time goes in v1:
time: 305 us
  waiting for transfers between devices  132 us (43%)
  blocking collectives  93.4 us (31%)
  local copies, waits for them, and re-layouts  58.9 us (19%)
  between operations  14.9 us (5%)
  other arithmetic  5.71 us (2%)
    unnamed x2, waiting for transfers between devices  132 us
    all_to_all x1, blocking collectives, swapped_in(): blocks = lax.all_to_all(blocks, name, split_axis=0, concat_axis=0)  93.4 us
    unnamed x43, local copies, waits for them, and re-layouts  20.1 us
    reshape x2, local copies, waits for them, and re-layouts, sum_together(): lines = jnp.concatenate([b.reshape(size, -1) for b in parts], axis=1)  10.8 us
    pad x1, local copies, waits for them, and re-layouts, sum_together(): jnp.pad(lines, ((0, 0), (0, width * 128 - lines.shape[1]))).reshape(-1, 128)  6.35 us
  transfers between devices with their start and end apart: 1, of which 1 were waited for; matrix products, arithmetic and copies ran while one was open for 0% of the time, Pallas kernels for 0%

profile of v1, /device:TPU:1, one launch (start us, length us, event | category | flops | bytes accessed | tf_op | source)
XLA Modules:
  0.0 304.8 jit_solution(17772197035838127383)
XLA Ops:
  7.2 1.9 reshape_reshape_squeeze.12
  9.1 1.5 constant_dynamic-update-slice_fusion.6
  10.6 2.0 copy.71
  12.7 4.1 %copy.72 = f32[16,768,48]{2,1,0:T(8,128)} copy(f32[16,768,48]{1,2,0:T(8,128)S(1)} %bitcast.23) | data formatting | bytes 4718592 | tf_op jit(solution)/shard_map/transpose | solution.py:19
  16.7 7.3 %reshape.81 = f32[16,36864]{1,0:T(8,128)S(1)} reshape(f32[16,768,48]{2,1,0:T(8,128)} %copy.72) | data formatting | bytes 4718592 | tf_op jit(solution)/shard_map/reshape | solution.py:25
  24.1 1.3 copy.73
  25.4 1.1 reshape_reshape_squeeze.13
  26.6 1.3 copy.74
  27.9 1.1 reshape_reshape_squeeze.14
  29.0 1.3 copy.75
  30.3 1.1 reshape_reshape_squeeze.15
  31.5 1.3 copy.76
  32.8 1.7 copy.77
  34.5 3.5 %reshape.82 = f32[16,9216]{1,0:T(8,128)} reshape(f32[16,192,48]{2,1,0:T(8,128)} %copy.77) | data formatting | bytes 1179648 | tf_op jit(solution)/shard_map/reshape | solution.py:25
  38.1 1.6 constant_dynamic-update-slice_fusion.5
  39.6 0.9 constant_dynamic-update-slice_fusion.4
  40.5 0.9 constant_dynamic-update-slice_fusion.3
  41.4 0.9 constant_dynamic-update-slice_fusion.2
  42.3 0.9 constant_dynamic-update-slice_fusion.1
  43.1 0.6 constant_dynamic-update-slice_fusion
  43.7 6.4 %pad.4 = f32[16,111616]{1,0:T(8,128)} pad(f32[16,110640]{1,0:T(8,128)} %constant_dynamic-update-slice_fusion, f32[]{:T(128)} %constant.8.clone.1), padding=0_0x0_976 | pad | bytes 14224388 | tf_op jit(solution)/shard_map/jit(_pad)/pad | solution.py:27
  50.1 5.5 %reshape.83 = f32[13952,128]{1,0:T(8,128)} reshape(f32[16,111616]{1,0:T(8,128)} %pad.4) | data formatting | bytes 14286848 | tf_op jit(solution)/shard_map/reshape | solution.py:27
  55.6 0.6 copy-done.12
  56.2 0.6 dynamic-slice
  57.5 132.0 %all-reduce.4.cloned.1.call-done = f32[13952,128]{1,0:T(8,128)} async-done(((f32[13952,128]{1,0:T(8,128)}), f32[13952,128]{1,0:T(8,128)}) %all-reduce.4.cloned.1.call-update) | async-done | bytes 7143440
  189.4 1.0 dynamic-slice_multiply_fusion
  190.5 0.2 mul.64
  190.7 0.1 copy.78
  190.8 0.9 dynamic-slice_multiply_fusion.2
  192.1 1.1 dynamic-slice_bitcast_fusion
  193.2 0.5 convert_bitcast_fusion.2
  193.7 0.1 copy.80
  193.8 0.7 fusion.5
  194.5 0.7 convert_bitcast_fusion
  195.2 0.6 fusion.4
  195.8 0.6 convert_bitcast_fusion.1
  196.4 0.6 fusion.2
  197.1 0.1 concatenate.7
  197.2 0.3 stack.2
  197.4 93.4 %all_to_all.5 = bf16[16,48,2305]{2,1,0:T(8,128)(2,1)S(1)} all-to-all(bf16[16,48,2305]{2,1,0:T(8,128)(2,1)S(1)} %stack.2), channel_id=1, replica_groups=mesh['unit'=4,'replica'=16,'model'=4] {'replica'}, dimensions={0} | all-to-all | bytes 7080960 | tf_op jit(solution)/shard_map/all_to_all | solution.py:12
  290.8 1.2 slice_bitcast_fusion
  292.0 0.4 slice_bitcast_fusion.1
  292.3 0.7 slice_reduce_fusion
  293.1 1.4 copy.81
  294.5 0.9 copy.82
  295.4 0.9 copy.83
  296.3 0.9 copy.84
  297.1 0.9 copy.85
  (35 shorter events, 0.6 us)
Async XLA Ops:
  7.2 182.2 %all-reduce.4.cloned.1.call-start = ((), (), s32[]{:S(2)}) async-start(), calls=%async_computation.1 | async-start | bytes 14286848
  24.1 13.9 %copy-start.10 = (f32[1,768]{1,0:T(1,128)S(1)}, f32[1,768]{1,0:T(1,128)}, u32[]{:S(2)}) copy-start(f32[1,768]{1,0:T(1,128)} %param.20) | copy-start | bytes 9220
  34.5 5.2 %copy-start = (f32[16,9216]{1,0:T(8,128)S(1)}, f32[16,9216]{1,0:T(8,128)}, u32[]{:S(2)}) copy-start(f32[16,9216]{1,0:T(8,128)} %reshape_reshape_squeeze.13) | copy-start | bytes 1769476
  34.5 6.0 %copy-start.1 = (f32[16,9216]{1,0:T(8,128)S(1)}, f32[16,9216]{1,0:T(8,128)}, u32[]{:S(2)}) copy-start(f32[16,9216]{1,0:T(8,128)} %reshape_reshape_squeeze.14) | copy-start | bytes 1769476
  38.1 3.3 %copy-start.2 = (f32[16,9216]{1,0:T(8,128)S(1)}, f32[16,9216]{1,0:T(8,128)}, u32[]{:S(2)}) copy-start(f32[16,9216]{1,0:T(8,128)} %reshape_reshape_squeeze.15) | copy-start | bytes 1769476
  38.1 4.2 %copy-start.3 = (f32[16,9216]{1,0:T(8,128)S(1)}, f32[16,9216]{1,0:T(8,128)}, u32[]{:S(2)}) copy-start(f32[16,9216]{1,0:T(8,128)} %reshape.82) | copy-start | bytes 1769476
  55.5 0.7 copy-start.12
  55.5 137.6 %copy-start.11 = (f32[48]{0:T(128)S(1)}, f32[48]{0:T(128)}, u32[]{:S(2)}) copy-start(f32[48]{0:T(128)} %param.27) | copy-start | bytes 580
  55.5 138.3 %copy-start.4 = (f32[48,768]{1,0:T(8,128)S(1)}, f32[48,768]{1,0:T(8,128)}, u32[]{:S(2)}) copy-start(f32[48,768]{1,0:T(8,128)} %param.21) | copy-start | bytes 442372
  55.5 138.9 %copy-start.5 = (f32[768,48]{0,1:T(8,128)S(1)}, f32[768,48]{0,1:T(8,128)}, u32[]{:S(2)}) copy-start(f32[768,48]{0,1:T(8,128)} %param.22) | copy-start | bytes 442372
  55.6 139.6 %copy-start.6 = (f32[48,192]{1,0:T(8,128)S(1)}, f32[48,192]{1,0:T(8,128)}, u32[]{:S(2)}) copy-start(f32[48,192]{1,0:T(8,128)} %param.23) | copy-start | bytes 110596
  55.6 140.2 %copy-start.7 = (f32[192,48]{0,1:T(8,128)S(1)}, f32[192,48]{0,1:T(8,128)}, u32[]{:S(2)}) copy-start(f32[192,48]{0,1:T(8,128)} %param.26) | copy-start | bytes 110596
  55.6 140.8 %copy-start.8 = (f32[48,192]{1,0:T(8,128)S(1)}, f32[48,192]{1,0:T(8,128)}, u32[]{:S(2)}) copy-start(f32[48,192]{1,0:T(8,128)} %param.25) | copy-start | bytes 110596
  55.6 140.8 %copy-start.9 = (f32[48,192]{1,0:T(8,128)S(1)}, f32[48,192]{1,0:T(8,128)}, u32[]{:S(2)}) copy-start(f32[48,192]{1,0:T(8,128)} %param.24) | copy-start | bytes 110596
Sparse Core Ops, SparseCore 0:
  55.8 133.6 all-reduce.3
